TPU v7x, 32 devices: a whole 2x2x4 slice. The times are simulated.
32 devices in a mesh: dp: 8 (over y, x, core), tensor: 4 (over z).
Axes of the slice: x: 2, y: 2, z: 4, core: 2. Of those that a mesh axis runs over, the one named last changes fastest.
Arguments:
- tokens: bfloat16 [256, 6144], P('dp', 'tensor'), may hold values from -6 to 6
- router_weight: bfloat16 [6144, 8], P('tensor'), may hold values from -0.078125 to 0.078125
- expert_ids: int32 [256, 2], P('dp'), may hold values from 0 to 7, all different within a row; in each aligned block of 32 rows (0 to 31, 32 to 63, ...) at most 12 rows name the same one
- w_gate: bfloat16 [8, 6144, 12288], P('dp', None, 'tensor'), may hold values from -0.078125 to 0.078125
- w_up: bfloat16 [8, 6144, 12288], P('dp', None, 'tensor'), may hold values from -0.078125 to 0.078125
- w_down: bfloat16 [8, 12288, 6144], P('dp', 'tensor'), may hold values from -0.0546875 to 0.0546875
Outputs:
- moe_out: bfloat16 [256, 6144], P('dp', 'tensor')
Inputs may be any that keep to these rules, and one draw needn't show every extreme that they name: `expert_ids`: the two experts of a token differ. In each aligned block of 32 rows (the rows of one index of dp) no expert is named by more than 12 rows, a bound that some blocks reach.
All inputs are finite; a program needn't handle non-finite values.
Results may differ from a plain program's by a relative error of at most 0.022.
Values may be sent and summed in bfloat16 or wider, within the bound.
A program may use at most 192 MiB of HBM per device.

v0:
```python
import jax
import jax.numpy as jnp
from jax import lax
from jax.sharding import PartitionSpec as P

EXPERTS = 8
CAP = 12


def per_device(tokens, router_weight, expert_ids, w_gate, w_up, w_down):
    tok_rows = tokens.shape[0]
    share = tokens.shape[1]
    dp_count = lax.axis_size("dp")
    groups = dp_count // EXPERTS
    slot_count = EXPERTS * CAP
    partial_value = jnp.dot(tokens, router_weight, preferred_element_type=jnp.float32)
    logits = lax.psum(partial_value, "tensor")
    choose = (expert_ids[:, :, None] == jnp.arange(EXPERTS, dtype=jnp.int32)[None, None, :]).astype(
        jnp.float32
    )
    chosen = jnp.sum(choose * logits[:, None, :], axis=2)
    first = jax.nn.sigmoid(chosen[:, 0] - chosen[:, 1])
    gates = jnp.stack([first, 1.0 - first], axis=1)
    flat = expert_ids.reshape(-1)
    onehot = (flat[:, None] == jnp.arange(EXPERTS, dtype=jnp.int32)[None, :]).astype(jnp.int32)
    ranks = jnp.sum((jnp.cumsum(onehot, axis=0) - onehot) * onehot, axis=1)
    position = flat * CAP + ranks
    slot_table = (position[:, None] == jnp.arange(slot_count, dtype=jnp.int32)[None, :]).astype(
        jnp.float32
    )
    slot_table = slot_table.reshape(tok_rows, 2, slot_count)
    placing = jnp.sum(slot_table, axis=1).astype(jnp.bfloat16)
    weights = jnp.sum(slot_table * gates[:, :, None], axis=1)
    packed = lax.dot_general(
        placing, tokens, (((0,), (0,)), ((), ())), preferred_element_type=jnp.float32
    ).astype(jnp.bfloat16)
    outgoing = jnp.broadcast_to(
        packed.reshape(EXPERTS, 1, CAP, share), (EXPERTS, groups, CAP, share)
    ).reshape(dp_count, CAP, share)
    incoming = lax.all_to_all(outgoing, "dp", split_axis=0, concat_axis=0, tiled=True)
    rows = incoming.reshape(dp_count * CAP, share)
    gate_w = w_gate[0]
    up_w = w_up[0]
    down_w = w_down[0]
    whole = lax.all_gather(rows, "tensor", axis=1, tiled=True)
    gate = jnp.dot(whole, gate_w, preferred_element_type=jnp.float32)
    up = jnp.dot(whole, up_w, preferred_element_type=jnp.float32)
    hidden = (jax.nn.silu(gate) * up).astype(jnp.bfloat16)
    terms = jnp.dot(hidden, down_w, preferred_element_type=jnp.float32)
    summed = lax.psum_scatter(terms.astype(jnp.bfloat16), "tensor", scatter_dimension=1, tiled=True)
    leaving = summed.reshape(dp_count, CAP, share)
    back = lax.all_to_all(leaving, "dp", split_axis=0, concat_axis=0, tiled=True)
    merged = jnp.sum(back.astype(jnp.float32).reshape(EXPERTS, groups, CAP, share), axis=1).reshape(
        slot_count, share
    )
    result = jnp.dot(
        weights, merged, precision=lax.Precision.HIGHEST, preferred_element_type=jnp.float32
    )
    return result.astype(jnp.bfloat16)


def solution(mesh):
    return jax.shard_map(
        per_device,
        mesh=mesh,
        in_specs=(
            P("dp", "tensor"),
            P("tensor", None),
            P("dp", None),
            P("dp", None, "tensor"),
            P("dp", None, "tensor"),
            P("dp", "tensor", None),
        ),
        out_specs=P("dp", "tensor"),
        check_vma=False,
    )
```

profile of v0, /device:TPU:0, one launch (start us, length us, event | category | flops | bytes accessed | tf_op | source)
XLA Modules:
  0.0 160.2 jit_solution(1804313521024078486)
XLA Ops:
  6.5 0.0 copy-start
  6.5 0.0 all-gather.2.cloned.1.call-start
  6.5 0.9 copy-done
  7.4 0.9 fusion.21
  8.3 13.5 %psum.7 = f32[32,8]{0,1:T(8,128)S(1)} all-reduce(f32[32,8]{0,1:T(8,128)S(1)} %fusion.21), channel_id=1, replica_groups=mesh['dp'=8,'tensor'=4] {'tensor'}, use_global_device_ids=true, to_apply=%region_2.0 | all-reduce | flops 256 | bytes 2048 | tf_op jit(solution)/shard_map/psum | solution.py:17
  21.8 0.8 copy.27
  22.5 0.7 select_reduce_fusion.2
  23.2 0.1 eq.42
  23.3 0.1 fusion.18
  23.4 0.1 reduce_window_sum.11
  23.5 0.2 select_reduce_fusion.1
  23.7 0.1 reduce_sum.43
  23.8 0.1 copy.28
  23.9 0.7 multiply_add_fusion
  24.6 0.1 convert_reduce_fusion
  24.7 0.3 convolution_convert_fusion
  25.0 0.1 reshape_reshape.3
  25.0 11.8 %all_to_all.10 = bf16[8,12,1536]{2,1,0:T(8,128)(2,1)S(1)} all-to-all(bf16[8,12,1536]{2,1,0:T(8,128)(2,1)S(1)} %reshape_reshape.3), channel_id=1, replica_groups=mesh['dp'=8,'tensor'=4] {'dp'}, dimensions={0} | all-to-all | bytes 589824 | tf_op jit(solution)/shard_map/all_to_all | solution.py:40
  36.8 0.8 reshape.35
  37.6 0.0 all-gather.2.cloned.1.call-update
  37.7 0.0 reduce-scatter.2.cloned.1.call-start
  37.7 26.7 %all-gather.2.cloned.1.call-done = bf16[96,6144]{1,0:T(8,128)(2,1)} async-done(((bf16[96,1536]{1,0:T(8,128)(2,1)}), bf16[96,6144]{1,0:T(8,128)(2,1)}) %all-gather.2.cloned.1.call-update) | async-done | bytes 1179664 | tf_op jit(solution)/shard_map/all_gather | solution.py:45
  64.4 18.4 %fusion.4 = f32[96,3072]{1,0:T(8,128)S(1)} fusion(bf16[96,6144]{1,0:T(8,128)(2,1)} %all-gather.2.cloned.1.call-done, bf16[1,6144,3072]{2,1,0:T(8,128)(2,1)} %param.9), kind=kOutput, calls=%fused_computation.4 | convolution fusion | flops 3623878656 | bytes 40108032 | tf_op jit(solution)/shard_map/dot_general | solution.py:46
  82.8 0.0 copy-done.2
  82.8 28.1 %fusion.6 = bf16[96,6144]{1,0:T(8,128)(2,1)} fusion(bf16[1,3072,6144]{2,1,0:T(8,128)(2,1)} %param.11, bf16[96,6144]{1,0:T(8,128)(2,1)S(1)} %copy-done.2, bf16[1,6144,3072]{2,1,0:T(8,128)(2,1)} %param.10, f32[96,3072]{1,0:T(8,128)S(1)} %fusion.4), kind=kOutput, calls=%fused_computation.6 | convolution fusion | flops 7250116608 | bytes 79036416 | tf_op jit(solution)/shard_map/dot_general | solution.py:49
  110.9 0.0 reduce-scatter.2.cloned.1.call-update
  110.9 0.0 copy-start.1
  110.9 28.7 %reduce-scatter.2.cloned.1.call-done = bf16[96,1536]{1,0:T(8,128)(2,1)} async-done(((bf16[96,6144]{1,0:T(8,128)(2,1)}), bf16[96,1536]{1,0:T(8,128)(2,1)}) %reduce-scatter.2.cloned.1.call-update) | async-done | bytes 294928 | tf_op jit(solution)/shard_map/reduce_scatter | solution.py:50
  139.6 1.0 reshape.36
  140.7 11.8 %all_to_all.11 = bf16[8,12,1536]{2,1,0:T(8,128)(2,1)S(1)} all-to-all(bf16[8,12,1536]{2,1,0:T(8,128)(2,1)S(1)} %reshape.36), channel_id=1, replica_groups=mesh['dp'=8,'tensor'=4] {'dp'}, dimensions={0} | all-to-all | bytes 589824 | tf_op jit(solution)/shard_map/all_to_all | solution.py:52
  152.4 0.1 reshape.37
  152.5 0.9 convolution_convert_fusion.1
  (4 shorter events, 0.0 us)
Async XLA Ops:
  6.5 0.9 copy-start
  6.5 57.9 %all-gather.2.cloned.1.call-start = ((), (), s32[]{:S(2)}) async-start(), calls=%async_computation.3 | async-start | bytes 1474560 | tf_op jit(solution)/shard_map/all_gather | solution.py:45
  37.7 102.0 %reduce-scatter.2.cloned.1.call-start = ((), (), s32[]{:S(2)}) async-start(), calls=%async_computation.4 | async-start | bytes 1474560 | tf_op jit(solution)/shard_map/reduce_scatter | solution.py:50
  64.4 18.4 %copy-start.2 = (bf16[96,6144]{1,0:T(8,128)(2,1)S(1)}, bf16[96,6144]{1,0:T(8,128)(2,1)}, u32[]{:S(2)}) copy-start(bf16[96,6144]{1,0:T(8,128)(2,1)} %all-gather.2.cloned.1.call-done) | copy-start | bytes 3538948
  110.9 42.5 %copy-start.1 = (bf16[32,1536]{1,0:T(8,128)(2,1)S(1)}, bf16[32,1536]{1,0:T(8,128)(2,1)}, u32[]{:S(2)}) copy-start(bf16[32,1536]{1,0:T(8,128)(2,1)} %param.6) | copy-start | bytes 294916
Sparse Core Ops, SparseCore 0:
  37.8 26.5 all-gather.1
  111.0 28.5 reduce-scatter.1
where the time goes:
time: 161 us; the launch traced here: 160 us
  waiting for transfers between devices  55.4 us (34%)
  matrix products  48.5 us (30%)
  blocking collectives  37 us (23%)
  between operations  13.5 us (8%)
  local copies, waits for them, and re-layouts  3.9 us (2%)
  other arithmetic  1.85 us (1%)
    reduce_scatter x1, waiting for transfers between devices, per_device(): lax.psum_scatter(terms.astype(jnp.bfloat16), 'tensor', scatter_dimension=...  28.7 us
    dot_general x1, matrix products, per_device(): terms = jnp.dot(hidden, down_w, preferred_element_type=jnp.float32)  28.1 us
    all_gather x1, waiting for transfers between devices, per_device(): whole = lax.all_gather(rows, 'tensor', axis=1, tiled=True)  26.7 us
    dot_general x1, matrix products, per_device(): gate = jnp.dot(whole, gate_w, preferred_element_type=jnp.float32)  18.4 us
    psum x1, blocking collectives, per_device(): logits = lax.psum(partial_value, 'tensor')  13.5 us
    all_to_all x1, blocking collectives, per_device(): lax.all_to_all(outgoing, 'dp', split_axis=0, concat_axis=0, tiled=True)  11.8 us
    all_to_all x1, blocking collectives, per_device(): lax.all_to_all(leaving, 'dp', split_axis=0, concat_axis=0, tiled=True)  11.8 us
  transfers between devices with their start and end apart: 2, of which 2 were waited for; matrix products, arithmetic and copies ran while one was open for 0% of the time, Pallas kernels for 0%

commit v1 on v0

v1 whole, which is shorter than its diff:
```python
import functools

import jax
import jax.numpy as jnp
from jax import lax
from jax.experimental import pallas as pl
from jax.experimental.pallas import tpu as pltpu
from jax.sharding import PartitionSpec as P

EXPERTS = 8
CAP = 12
PAD = 16
LAG = 4
SLOTS = 16
F32 = jnp.float32
BF16 = jnp.bfloat16


def body(dp, nt, n, sub, pps, slots, tok_ref, rw_ref, ids_ref, wg_ref, wu_ref, wd_ref, out_ref,
         wbuf, rows, packed, hidden, ret_out, ret_in, ztok, zout, zin, own, lg_out, lg_in, hits, wmat,
         w_sem, zt_send, zt_recv, lg_send, lg_recv, d_send, d_recv, r_send, r_recv, zo_send, zo_recv):
    me = lax.axis_index("dp")
    t = lax.axis_index("tensor")
    toks, share = tok_ref.shape
    depth, ff = wg_ref.shape
    width = dp * PAD
    groups = dp // EXPERTS
    chunks = ff // n
    cb = pps * n
    steps = nt * sub
    units = 2 * chunks + steps
    mesh = pl.DeviceIdType.MESH

    def column(s):
        zi = s // sub
        half = nt // 2
        off = jnp.where(zi % 2 == 0, half - zi // 2, half + (zi + 1) // 2)
        q = lax.rem(t + off, nt)
        return q, s % sub

    def load(u, act):
        slot = lax.rem(u, slots)

        @pl.when(u < 2 * chunks)
        def _():
            cols = pl.ds(pl.multiple_of((u // 2) * n, n), n)

            @pl.when(u % 2 == 0)
            def _():
                act(pltpu.make_async_copy(wg_ref.at[:, cols], wbuf.at[slot], w_sem.at[slot]))

            @pl.when(u % 2 == 1)
            def _():
                act(pltpu.make_async_copy(wu_ref.at[:, cols], wbuf.at[slot], w_sem.at[slot]))

        @pl.when((u >= 2 * chunks) & (u < units))
        def _():
            q, j = column(u - 2 * chunks)
            for k in range(pps):
                cols = pl.ds(pl.multiple_of(q * share + j * cb + k * n, n), n)
                act(pltpu.make_async_copy(
                    wd_ref.at[:, cols], wbuf.at[slot, pl.ds(k * ff, ff)], w_sem2(slot, k)))

    def w_sem2(slot, k):
        return w_sem.at[k * slots + slot]

    @pl.loop(0, min(slots, units))
    def _(u):
        load(u, lambda c: c.start())

    rows[...] = jnp.zeros_like(rows)
    ret_in[...] = jnp.zeros_like(ret_in)
    barrier = pltpu.get_barrier_semaphore()

    @pl.loop(1, dp)
    def _(i):
        pl.semaphore_signal(barrier, inc=1, device_id={"dp": lax.rem(me + i, dp)}, device_id_type=mesh)

    @pl.loop(1, nt)
    def _(i):
        pl.semaphore_signal(barrier, inc=1, device_id={"tensor": lax.rem(t + i, nt)}, device_id_type=mesh)

    pl.semaphore_wait(barrier, dp + nt - 2)

    @pl.loop(1, nt)
    def _(i):
        pltpu.make_async_remote_copy(
            tok_ref, ztok.at[t], zt_send.at[i], zt_recv.at[t],
            device_id={"tensor": lax.rem(t + i, nt)}, device_id_type=mesh).start()

    ids = ids_ref[...]
    lane = lax.broadcasted_iota(jnp.int32, (toks, width), 1)
    expert = lane // (PAD * groups)
    rank = (lane % PAD).astype(F32)
    named = [ids[:, k:k + 1] == expert for k in range(2)]
    counts = (named[0] | named[1]).astype(F32).astype(BF16)
    lower = (lax.broadcasted_iota(jnp.int32, (toks, toks), 0)
             > lax.broadcasted_iota(jnp.int32, (toks, toks), 1)).astype(F32).astype(BF16)
    before = jnp.dot(lower, counts, preferred_element_type=F32)
    at_rank = before == rank
    for k in range(2):
        hits[k] = (named[k] & at_rank).astype(F32)
    placing = ((named[0] | named[1]) & at_rank).astype(F32)

    def dispatch(src, value):
        cols = pl.ds(pl.multiple_of(src * share, share), share)
        block = lax.dot_general(placing.astype(BF16), value, (((0,), (0,)), ((), ())),
                                preferred_element_type=F32).astype(BF16)
        packed[src] = block.reshape(dp, PAD, share)
        rows[me, :, cols] = packed[src, me]

        @pl.loop(1, dp)
        def _(i):
            p = lax.rem(me + i, dp)
            pltpu.make_async_remote_copy(
                packed.at[src, p, pl.ds(0, PAD)], rows.at[me, pl.ds(0, PAD), cols],
                d_send.at[src], d_recv.at[src],
                device_id={"dp": p}, device_id_type=mesh).start()

    dispatch(t, tok_ref[...])
    lg_out[...] = jnp.zeros_like(lg_out)
    lg_out[:, 0:EXPERTS] = jnp.dot(tok_ref[...], rw_ref[...], preferred_element_type=F32)
    lg_in[t] = lg_out[...]

    @pl.loop(1, nt)
    def _(i):
        pltpu.make_async_remote_copy(
            lg_out, lg_in.at[t], lg_send.at[i], lg_recv.at[t],
            device_id={"tensor": lax.rem(t + i, nt)}, device_id_type=mesh).start()

    @pl.loop(1, nt)
    def _(i):
        src = lax.rem(t + jnp.where(i % 2 == 1, nt - (i + 1) // 2, i // 2), nt)
        pltpu.make_async_copy(ztok.at[src], ztok.at[src], zt_recv.at[src]).wait()
        dispatch(src, ztok[src])

    @pl.loop(1, nt)
    def _(i):
        src = lax.rem(t + i, nt)
        pltpu.make_async_copy(lg_in.at[src], lg_in.at[src], lg_recv.at[src]).wait()

    logits = jnp.sum(lg_in[...], axis=0)
    lane8 = lax.broadcasted_iota(jnp.int32, logits.shape, 1)
    chosen = [jnp.sum(jnp.where(lane8 == ids[:, k:k + 1], logits, 0.0), axis=1, keepdims=True)
              for k in range(2)]
    first = jax.nn.sigmoid(chosen[0] - chosen[1])
    w = hits[0] * first + hits[1] * (1.0 - first)
    for k in range(3):
        part = w.astype(BF16)
        wmat[k] = part
        w = w - part.astype(F32)

    @pl.loop(0, nt)
    def _(src):
        cols = pl.ds(pl.multiple_of(src * share, share), share)
        view = rows.at[pl.ds(0, dp - 1), pl.ds(0, PAD), cols]
        pltpu.make_async_copy(view, view, d_recv.at[src]).wait()

    @pl.loop(0, chunks)
    def _(c):
        vals = []
        for k in range(2):
            u = 2 * c + k
            slot = lax.rem(u, slots)
            pltpu.make_async_copy(wbuf.at[slot], wbuf.at[slot], w_sem.at[slot]).wait()
            vals.append(jnp.dot(rows[...].reshape(width, depth), wbuf[slot], preferred_element_type=F32))
            load(u + slots, lambda d: d.start())
        gate, up = vals
        hidden[:, pl.ds(pl.multiple_of(c * n, n), n)] = (gate / (1.0 + jnp.exp(-gate)) * up).astype(BF16)

    @pl.loop(0, steps + LAG)
    def _(s):
        @pl.when(s < steps)
        def _():
            u = 2 * chunks + s
            slot = lax.rem(u, slots)
            load(u, lambda d: d.wait())
            for k in range(pps):
                term = jnp.dot(hidden[...], wbuf[slot, pl.ds(k * ff, ff)], preferred_element_type=F32)
                ret_out[s, :, :, pl.ds(k * n, n)] = term.astype(BF16).reshape(dp, PAD, n)
            load(u + slots, lambda d: d.start())
            ret_in[s, me] = ret_out[s, me]

            @pl.loop(1, dp)
            def _(i):
                p = lax.rem(me + i, dp)
                pltpu.make_async_remote_copy(
                    ret_out.at[s, p, pl.ds(0, PAD)], ret_in.at[s, me, pl.ds(0, PAD)],
                    r_send.at[s], r_recv.at[s],
                    device_id={"dp": p}, device_id_type=mesh).start()

        @pl.when(s >= LAG)
        def _():
            b = s - LAG
            q, j = column(b)
            view = ret_in.at[b, pl.ds(0, dp - 1), pl.ds(0, PAD)]
            pltpu.make_async_copy(view, view, r_recv.at[b]).wait()
            back = ret_in[b].reshape(width, cb)
            mixed = jnp.dot(wmat[0], back, preferred_element_type=F32)
            for k in range(1, 3):
                mixed += jnp.dot(wmat[k], back, preferred_element_type=F32)

            @pl.when(b < steps - sub)
            def _():
                zout[b] = mixed.astype(BF16)
                pltpu.make_async_remote_copy(
                    zout.at[b], zin.at[t, j], zo_send.at[b], zo_recv.at[t * sub + j],
                    device_id={"tensor": q}, device_id_type=mesh).start()

            @pl.when(b >= steps - sub)
            def _():
                own[j] = mixed

    @pl.loop(1, nt)
    def _(i):
        src = lax.rem(t + i, nt)

        @pl.loop(0, sub)
        def _(j):
            pltpu.make_async_copy(zin.at[src, j], zin.at[src, j], zo_recv.at[src * sub + j]).wait()
            own[j] += zin[src, j].astype(F32)

    for j in range(sub):
        out_ref[:, j * cb:(j + 1) * cb] = own[j].astype(BF16)

    @pl.loop(1, nt)
    def _(i):
        pltpu.make_async_copy(tok_ref, tok_ref, zt_send.at[i]).wait()
        pltpu.make_async_copy(lg_out, lg_out, lg_send.at[i]).wait()

    @pl.loop(0, nt)
    def _(src):
        view = packed.at[src, pl.ds(0, dp - 1), pl.ds(0, PAD)]
        pltpu.make_async_copy(view, view, d_send.at[src]).wait()

    @pl.loop(0, steps)
    def _(s):
        view = ret_out.at[s, pl.ds(0, dp - 1), pl.ds(0, PAD)]
        pltpu.make_async_copy(view, view, r_send.at[s]).wait()

    @pl.loop(0, steps - sub)
    def _(s):
        pltpu.make_async_copy(zout.at[s], zout.at[s], zo_send.at[s]).wait()


def per_device(dp, nt, tokens, router_weight, expert_ids, w_gate, w_up, w_down):
    toks, share = tokens.shape
    _, depth, ff = w_gate.shape
    n = min(256, ff)
    sub = 1
    while share // (sub * n) * ff > depth or share % (sub * n):
        sub += 1
    pps = share // (sub * n)
    cb = pps * n
    steps = nt * sub
    width = dp * PAD
    slots = SLOTS
    dma = pltpu.SemaphoreType.DMA
    vm = pl.BlockSpec(memory_space=pltpu.VMEM)
    hbm = pl.BlockSpec(memory_space=pltpu.HBM)
    return pl.pallas_call(
        functools.partial(body, dp, nt, n, sub, pps, slots),
        out_shape=jax.ShapeDtypeStruct((toks, share), BF16),
        in_specs=[vm, vm, vm, hbm, hbm, hbm],
        out_specs=vm,
        scratch_shapes=[
            pltpu.VMEM((slots, depth, n), BF16),
            pltpu.VMEM((dp, PAD, depth), BF16),
            pltpu.VMEM((nt, dp, PAD, share), BF16),
            pltpu.VMEM((width, ff), BF16),
            pltpu.VMEM((steps, dp, PAD, cb), BF16),
            pltpu.VMEM((steps, dp, PAD, cb), BF16),
            pltpu.VMEM((nt, toks, share), BF16),
            pltpu.VMEM((steps, toks, cb), BF16),
            pltpu.VMEM((nt, sub, toks, cb), BF16),
            pltpu.VMEM((sub, toks, cb), F32),
            pltpu.VMEM((toks, 128), F32),
            pltpu.VMEM((nt, toks, 128), F32),
            pltpu.VMEM((2, toks, width), F32),
            pltpu.VMEM((3, toks, width), BF16),
            dma((slots * pps,)),
            dma((nt,)), dma((nt,)), dma((nt,)), dma((nt,)),
            dma((nt,)), dma((nt,)), dma((steps,)), dma((steps,)),
            dma((steps,)), dma((steps,)),
        ],
        compiler_params=pltpu.CompilerParams(
            collective_id=0, has_side_effects=True, vmem_limit_bytes=67043328),
    )(tokens, router_weight, expert_ids, w_gate[0], w_up[0], w_down[0])


def solution(mesh):
    return jax.shard_map(
        functools.partial(per_device, mesh.shape["dp"], mesh.shape["tensor"]),
        mesh=mesh,
        in_specs=(
            P("dp", "tensor"),
            P("tensor", None),
            P("dp", None),
            P("dp", None, "tensor"),
            P("dp", None, "tensor"),
            P("dp", "tensor", None),
        ),
        out_specs=P("dp", "tensor"),
        check_vma=False,
    )
```

time: 161 us -> 75.5 us (0.47)
  Pallas kernels: 0 us -> 70.7 us
  waiting for transfers between devices: 55.4 us -> 0 us
  matrix products: 48.5 us -> 0 us
  blocking collectives: 37 us -> 0 us
  between operations: 13.5 us -> 0.01 us
  other arithmetic: 1.85 us -> 0 us
    pallas_call x0 -> x1, Pallas kernels: none -> 70.7 us  [per_device(): pl.pallas_call(functools.partial(body, dp, nt, n, sub, pps, slots), out_s...]
    dot_general x5 -> x0, matrix products: 48.5 us -> none  [the longest x1 28.1 us: per_device(): terms = jnp.dot(hidden, down_w, preferred_element_type=jnp.float32)]
    reduce_scatter x1 -> x0, waiting for transfers between devices: 28.7 us -> none  [per_device(): lax.psum_scatter(terms.astype(jnp.bfloat16), 'tensor', scatter_dimension=...]
    all_gather x1 -> x0, waiting for transfers between devices: 26.7 us -> none  [per_device(): whole = lax.all_gather(rows, 'tensor', axis=1, tiled=True)]
    all_to_all x2 -> x0, blocking collectives: 23.6 us -> none  [the longest x1 11.8 us: per_device(): lax.all_to_all(outgoing, 'dp', split_axis=0, concat_axis=0, tiled=True)]
    psum x1 -> x0, blocking collectives: 13.5 us -> none  [per_device(): logits = lax.psum(partial_value, 'tensor')]
    unnamed x7 -> x3, local copies, waits for them, and re-layouts: 1.66 us -> 4.55 us
    reshape x3 -> x0, local copies, waits for them, and re-layouts: 1.88 us -> none  [the longest x1 1.03 us: per_device(): leaving = summed.reshape(dp_count, CAP, share)]
  transfers between devices with their start and end apart: 2 -> 0, of which waited for: 2 -> 0; matrix products, arithmetic and copies ran while one was open for 0% -> 0% of each run, Pallas kernels for 0% -> 0%
where the time goes in v1:
time: 75.5 us; the launch traced here: 75.3 us
  Pallas kernels  70.7 us (94%)
  local copies, waits for them, and re-layouts  4.55 us (6%)
    pallas_call x1, Pallas kernels, per_device(): pl.pallas_call(functools.partial(body, dp, nt, n, sub, pps, slots), out_s...  70.7 us
    unnamed x3, local copies, waits for them, and re-layouts  4.55 us

profile of v1, /device:TPU:0, one launch (start us, length us, event | category | flops | bytes accessed | tf_op | source)
XLA Modules:
  0.0 75.3 jit_solution(5413551305177722543)
XLA Ops:
  0.0 1.4 %copy.8.ids_ref = s32[32,2]{1,0:T(8,128)} copy(s32[32,2]{0,1:T(2,128)} %param.8) | data formatting | bytes 512 | tf_op args[2]
  1.4 1.6 %copy.7.rw_ref = bf16[1536,8]{1,0:T(8,128)(2,1)} copy(bf16[1536,8]{0,1:T(8,128)(2,1)} %param.7) | data formatting | bytes 49152 | tf_op args[1]
  3.0 70.7 %shard_map.64 = bf16[32,1536]{1,0:T(8,128)(2,1)} custom-call(bf16[32,1536]{1,0:T(8,128)(2,1)} %tok_ref.1, bf16[1536,8]{1,0:T(8,128)(2,1)} %copy.7.rw_ref, s32[32,2]{1,0:T(8,128)} %copy.8.ids_ref, bf16[6144,3072]{1,0:T(8,128)(2,1)} %bitcast.3, bf16[6144,3072]{1,0:T(8,128)(2,1)} %bitcast.4, bf16[3072,6144]{1,0:T(8,128)(2,1)} %bitcast.5), custom_call_target="tpu_custom_call" | custom-call | tf_op jit(solution)/shard_map/pallas_call | solution.py:261
  73.8 1.5 %copy.10 = bf16[32,1536]{1,0:T(8,128)(2,1)} copy(bf16[32,1536]{1,0:T(8,128)(2,1)} %shard_map.64) | data formatting | bytes 196608
